TPU v7x, 32 devices: a whole 2x2x4 slice. The times are simulated.
32 devices in a mesh: slab: 32 (over z, y, x, core).
Axes of the slice: x: 2, y: 2, z: 4, core: 2. Of those that a mesh axis runs over, the one named last changes fastest.
Arguments:
- points: float32 [4, 128, 128, 64], P(None, 'slab'), may hold values from -6 to 6
- offsets_x: int32 [256], replicated, may hold values from 0 to 124, as said below
- coeffs_x: float32 [4, 256], replicated, may hold values from 0.1 to 1
- offsets_y: int32 [256], replicated, may hold values from 0 to 124, as said below
- coeffs_y: float32 [4, 256], replicated, may hold values from 0.1 to 1
- offsets_z: int32 [128], replicated, may hold values from 0 to 60, as said below
- coeffs_z: float32 [4, 128], replicated, may hold values from 0.1 to 1
Outputs:
- refined: float32 [4, 256, 256, 128], P(None, None, 'slab')
Inputs may be any that keep to these rules, and one draw needn't show every extreme that they name: offsets_x[i] lies between i // 2 - 2 and i // 2, clipped to 0 .. 124. offsets_y[i] lies between i // 2 - 2 and i // 2, clipped to 0 .. 124. offsets_z[i] lies between i // 2 - 2 and i // 2, clipped to 0 .. 60.
All inputs are finite; a program needn't handle non-finite values.
Results may differ from a plain program's by a relative error of at most 0.000073.
Values sent between devices are 32-bit elements; how exact they have to be, the bound alone decides.
A program may use at most 64 MiB of HBM per device.

v0:
```python
import jax
import jax.numpy as jnp
from jax import lax
from jax.sharding import PartitionSpec as P


def band_matrix(offsets, coeffs, width, start):
    weights = coeffs / jnp.sum(coeffs, axis=0, keepdims=True)
    columns = jnp.arange(width, dtype=jnp.int32)[None, :]
    first = (offsets - start)[:, None]
    matrix = jnp.zeros((offsets.shape[0], width), jnp.float32)
    for k in range(4):
        matrix = matrix + jnp.where(columns == first + k, weights[k][:, None], 0.0)
    return matrix


def along_x(matrix, grid):
    return jnp.einsum("ia,cayz->ciyz", matrix, grid, precision=lax.Precision.HIGHEST)


def along_y(matrix, grid):
    return jnp.einsum("jb,cibz->cijz", matrix, grid, precision=lax.Precision.HIGHEST)


def along_z(matrix, grid):
    return jnp.einsum("le,cije->cijl", matrix, grid, precision=lax.Precision.HIGHEST)


def body(points, offsets_x, coeffs_x, offsets_y, coeffs_y, offsets_z, coeffs_z):
    coarse_y = points.shape[2]
    coarse_z = points.shape[3]
    matrix_y = band_matrix(offsets_y, coeffs_y, coarse_y, 0)
    matrix_z = band_matrix(offsets_z, coeffs_z, coarse_z, 0)
    grid = along_y(matrix_y, points)
    grid = lax.all_to_all(grid, "slab", split_axis=2, concat_axis=1, tiled=True)
    matrix_x = band_matrix(offsets_x, coeffs_x, grid.shape[1], 0)
    grid = along_x(matrix_x, grid)
    return along_z(matrix_z, grid)


def solution(mesh):
    return jax.shard_map(
        body,
        mesh=mesh,
        in_specs=(P(None, "slab", None, None), P(), P(), P(), P(), P(), P()),
        out_specs=P(None, None, "slab", None),
        check_vma=False,
    )
```

profile of v0, /device:TPU:0, one launch (start us, length us, event | category | flops | bytes accessed | tf_op | source)
XLA Modules:
  0.0 67.6 jit_solution(16214703891033774522)
XLA Ops:
  0.0 0.0 copy-start
  0.0 0.8 %reduce_sum.27 = f32[256]{0:T(256)S(1)} reduce(f32[4,256]{1,0:T(4,128)} %param.11, f32[]{:T(128)} %constant.4.clone.1), dimensions={0}, to_apply=%region_0.0 | reduce | flops 768 | bytes 5124 | tf_op jit(solution)/shard_map/reduce_sum | solution.py:8
  0.8 0.7 %broadcast_divide_fusion.1 = f32[4,256]{1,0:T(4,128)S(1)} fusion(f32[4,256]{1,0:T(4,128)} %param.11, f32[256]{0:T(256)S(1)} %reduce_sum.27), kind=kLoop, calls=%fused_computation.70 | loop fusion | flops 1024 | bytes 9216 | tf_op jit(solution)/shard_map/div | solution.py:8
  1.5 0.7 %broadcast_add_fusion.5 = (s32[256]{0:T(256)S(1)}, s32[256]{0:T(256)S(1)}, s32[256]{0:T(256)S(1)}) fusion(s32[256]{0:T(256)} %param.10), kind=kLoop, calls=%fused_computation.81 | loop fusion | flops 768 | bytes 4096 | tf_op jit(solution)/shard_map/add | solution.py:13
  2.2 0.0 copy-done
  2.2 2.9 %convolution_bitcast_fusion = f32[4,4,256,64]{2,3,1,0:T(8,128)} fusion(f32[4,4,128,64]{2,3,1,0:T(8,128)S(1)} %copy-done, f32[256]{0:T(256)S(1)} %bitcast.50, s32[256]{0:T(256)S(1)} %get-tuple-element.21, f32[256]{0:T(256)S(1)} %bitcast.51, s32[256]{0:T(256)S(1)} %get-tuple-element.22, f32[256]{0:T(256)S(1)} %bitcast.52, s32[256]{0:T(256)S(1)} %get-tuple-element.20, ...), kind=kOutput, calls=%fused_computation.5 | convolution fusion | flops 403013632 | bytes 1581056 | tf_op jit(solution)/shard_map/jb,cibz->cijz/dot_general | solution.py:22
  5.1 2.3 %copy.12 = f32[4,4,256,64]{3,1,0,2:T(4,128)S(1)} copy(f32[4,4,256,64]{2,3,1,0:T(8,128)} %convolution_bitcast_fusion) | data formatting | bytes 2097152 | tf_op jit(solution)/shard_map/jb,cibz->cijz/transpose | solution.py:22
  7.4 0.0 copy-start.2
  7.4 0.0 copy-start.1
  7.4 0.0 copy-start.4
  7.4 0.0 copy-start.3
  7.4 2.9 %reshape.39 = f32[32,1,8192]{2,1,0:T(1,128)} reshape(f32[256,4,4,64]{3,2,1,0:T(4,128)S(1)} %bitcast.45) | data formatting | bytes 2097152
  10.3 7.3 %all-to-all-start = ((f32[32,1,8192]{2,1,0:T(1,128)}), f32[32,1,8192]{2,1,0:T(1,128)S(1)}, u32[]{:S(2)}, u32[]{:S(2)}) async-start(f32[32,1,8192]{2,1,0:T(1,128)} %reshape.39), calls=%async_computation | async-start | bytes 2097152 | tf_op jit(solution)/shard_map/all_to_all | solution.py:35
  17.7 0.0 copy-done.2
  17.7 0.0 copy-done.1
  17.8 26.0 %all-to-all-done = f32[32,1,8192]{2,1,0:T(1,128)S(1)} async-done(((f32[32,1,8192]{2,1,0:T(1,128)}), f32[32,1,8192]{2,1,0:T(1,128)S(1)}, u32[]{:S(2)}, u32[]{:S(2)}) %all-to-all-start) | async-done | bytes 1048608 | tf_op jit(solution)/shard_map/all_to_all | solution.py:35
  43.9 0.5 broadcast.42
  44.4 4.4 %reduce = f32[32,8192]{1,0:T(8,128)} reduce(f32[32,1,8192]{2,1,0:T(1,128)S(1)} %all-to-all-done, f32[]{:T(128)} %broadcast.42), dimensions={1}, to_apply=%all_to_all.13.reduce_sub_computation | reduce | bytes 2097156 | tf_op jit(solution)/shard_map/all_to_all | solution.py:35
  48.8 2.8 %reshape.40 = f32[256,4,4,64]{3,2,1,0:T(4,128)S(1)} reshape(f32[32,8192]{1,0:T(8,128)} %reduce) | data formatting | bytes 2097152
  51.6 0.7 %copy.23 = f32[4,4,256,64]{3,2,1,0:T(8,128)S(1)} copy(f32[4,4,256,64]{3,1,0,2:T(4,128)S(1)} %bitcast.47) | data formatting | bytes 2097152 | tf_op jit(solution)/shard_map/all_to_all | solution.py:35
  52.3 0.3 copy.14
  52.6 3.8 %fusion.2 = f32[4,8,64,256]{3,2,1,0:T(8,128)S(1)} fusion(f32[4,128,8,64]{3,2,1,0:T(8,128)S(1)} %bitcast.46, f32[256]{0:T(256)S(1)} %bitcast.54, s32[256]{0:T(256)S(1)} %get-tuple-element.18, f32[256]{0:T(256)S(1)} %bitcast.55, s32[256]{0:T(256)S(1)} %get-tuple-element.19, f32[256]{0:T(256)S(1)} %bitcast.56, s32[256]{0:T(256)S(1)} %get-tuple-element.17, ...), kind=kOutput, calls=%fused_computation.2 | convolution fusion | flops 805666816 | bytes 3153920 | tf_op jit(solution)/shard_map/ia,cayz->ciyz/dot_general | solution.py:18
  56.4 6.8 %fusion = f32[4,256,8,128]{3,1,2,0:T(8,128)S(1)} fusion(f32[4,8,64,256]{3,2,1,0:T(8,128)S(1)} %fusion.2, f32[128]{0:T(128)S(1)} %get-tuple-element.14, s32[128]{0:T(128)S(1)} %get-tuple-element.24, f32[128]{0:T(128)S(1)} %get-tuple-element.15, s32[128]{0:T(128)S(1)} %get-tuple-element.25, f32[128]{0:T(128)S(1)} %get-tuple-element.16, ...), kind=kOutput, calls=%fused_computation | convolution fusion | flops 805396480 | bytes 6295552 | tf_op jit(solution)/shard_map/le,cije->cijl/dot_general | solution.py:26
  63.1 4.4 %copy.16 = f32[4,256,8,128]{3,2,1,0:T(8,128)} copy(f32[4,256,8,128]{3,1,2,0:T(8,128)S(1)} %fusion) | data formatting | bytes 8388608 | tf_op jit(solution)/shard_map/le,cije->cijl/dot_general | solution.py:26
  (11 shorter events, 0.1 us)
Async XLA Ops:
  0.0 2.2 %copy-start = (f32[4,4,128,64]{2,3,1,0:T(8,128)S(1)}, f32[4,4,128,64]{2,3,1,0:T(8,128)}, u32[]{:S(2)}) copy-start(f32[4,4,128,64]{2,3,1,0:T(8,128)} %param.7) | copy-start | bytes 1572868
  7.4 10.3 %copy-start.2 = (f32[4,128]{1,0:T(4,128)S(1)}, f32[4,128]{1,0:T(4,128)}, u32[]{:S(2)}) copy-start(f32[4,128]{1,0:T(4,128)} %param.13) | copy-start | bytes 6148
  7.4 10.3 %copy-start.1 = (f32[4,256]{1,0:T(4,128)S(1)}, f32[4,256]{1,0:T(4,128)}, u32[]{:S(2)}) copy-start(f32[4,256]{1,0:T(4,128)} %param.9) | copy-start | bytes 12292
  7.4 10.3 %copy-start.4 = (s32[128]{0:T(128)S(1)}, s32[128]{0:T(128)}, u32[]{:S(2)}) copy-start(s32[128]{0:T(128)} %param.12) | copy-start | bytes 1540
  7.4 10.3 %copy-start.3 = (s32[256]{0:T(256)S(1)}, s32[256]{0:T(256)}, u32[]{:S(2)}) copy-start(s32[256]{0:T(256)} %param.8) | copy-start | bytes 3076
  10.3 33.5 %all-to-all-start = ((f32[32,1,8192]{2,1,0:T(1,128)}), f32[32,1,8192]{2,1,0:T(1,128)S(1)}, u32[]{:S(2)}, u32[]{:S(2)}) async-start(f32[32,1,8192]{2,1,0:T(1,128)} %reshape.39), calls=%async_computation | async-start | bytes 2097152 | tf_op jit(solution)/shard_map/all_to_all | solution.py:35
where the time goes:
time: 67.9 us; the launch traced here: 67.6 us
  waiting for transfers between devices  26 us (38%)
  local copies, waits for them, and re-layouts  14 us (21%)
  matrix products  13.5 us (20%)
  starting transfers between devices  7.32 us (11%)
  other arithmetic  6.6 us (10%)
    all_to_all x1, waiting for transfers between devices, body(): grid = lax.all_to_all(grid, 'slab', split_axis=2, concat_axis=1, tiled=True)  26 us
    all_to_all x1, starting transfers between devices, body(): grid = lax.all_to_all(grid, 'slab', split_axis=2, concat_axis=1, tiled=True)  7.32 us
    dot_general x1, matrix products, along_z(): jnp.einsum('le,cije->cijl', matrix, grid, precision=lax.Precision.HIGHEST)  6.76 us
    unnamed x12, local copies, waits for them, and re-layouts  5.72 us
    dot_general x1, local copies, waits for them, and re-layouts, along_z(): jnp.einsum('le,cije->cijl', matrix, grid, precision=lax.Precision.HIGHEST)  4.44 us
    all_to_all x1, other arithmetic, body(): grid = lax.all_to_all(grid, 'slab', split_axis=2, concat_axis=1, tiled=True)  4.4 us
    dot_general x1, matrix products, along_x(): jnp.einsum('ia,cayz->ciyz', matrix, grid, precision=lax.Precision.HIGHEST)  3.79 us
    dot_general x1, matrix products, along_y(): jnp.einsum('jb,cibz->cijz', matrix, grid, precision=lax.Precision.HIGHEST)  2.95 us
  transfers between devices with their start and end apart: 1, of which 1 were waited for; matrix products, arithmetic and copies ran while one was open for 0% of the time, Pallas kernels for 0%

commit v1 on v0

--- a/solution.py
+++ b/solution.py
@@ -32,7 +32,15 @@
     matrix_y = band_matrix(offsets_y, coeffs_y, coarse_y, 0)
     matrix_z = band_matrix(offsets_z, coeffs_z, coarse_z, 0)
     grid = along_y(matrix_y, points)
-    grid = lax.all_to_all(grid, "slab", split_axis=2, concat_axis=1, tiled=True)
+    grid = jnp.concatenate(
+        lax.all_to_all(
+            jnp.stack(jnp.split(grid, lax.axis_size("slab"), 2), axis=0),
+            axis_name="slab",
+            split_axis=0,
+            concat_axis=0,
+        ),
+        1,
+    )
     matrix_x = band_matrix(offsets_x, coeffs_x, grid.shape[1], 0)
     grid = along_x(matrix_x, grid)
     return along_z(matrix_z, grid)

time: 67.9 us -> 138 us (2.03); the launches traced: 67.6 us -> 136 us
  local copies, waits for them, and re-layouts: 14 us -> 82.8 us
    another operation x0 -> x35, local copies, waits for them, and re-layouts: none -> 59.6 us  [body(): jnp.stack(jnp.split(grid, lax.axis_size('slab'), 2), axis=0)]
    unnamed x12 -> x61, local copies, waits for them, and re-layouts: 5.72 us -> 18 us
    transpose x1 -> x0, local copies, waits for them, and re-layouts: 2.29 us -> none  [along_y(): jnp.einsum('jb,cibz->cijz', matrix, grid, precision=lax.Precision.HIGHEST)]
where the time goes in v1:
time: 138 us; the launch traced here: 136 us
  local copies, waits for them, and re-layouts  82.8 us (60%)
  waiting for transfers between devices  25.9 us (19%)
  matrix products  12.5 us (9%)
  starting transfers between devices  7.5 us (5%)
  other arithmetic  6.6 us (5%)
    another operation x35, local copies, waits for them, and re-layouts, body(): jnp.stack(jnp.split(grid, lax.axis_size('slab'), 2), axis=0)  59.6 us
    all_to_all x1, waiting for transfers between devices, body(): lax.all_to_all(jnp.stack(jnp.split(grid, lax.axis_size('slab'), 2), axis=...  25.9 us
    unnamed x61, local copies, waits for them, and re-layouts  18 us
    all_to_all x1, starting transfers between devices, body(): lax.all_to_all(jnp.stack(jnp.split(grid, lax.axis_size('slab'), 2), axis=...  7.5 us
    dot_general x1, matrix products, along_z(): jnp.einsum('le,cije->cijl', matrix, grid, precision=lax.Precision.HIGHEST)  6.76 us
    dot_general x1, local copies, waits for them, and re-layouts, along_z(): jnp.einsum('le,cije->cijl', matrix, grid, precision=lax.Precision.HIGHEST)  4.44 us
    all_to_all x1, other arithmetic, body(): lax.all_to_all(jnp.stack(jnp.split(grid, lax.axis_size('slab'), 2), axis=...  4.4 us
    dot_general x1, matrix products, along_x(): jnp.einsum('ia,cayz->ciyz', matrix, grid, precision=lax.Precision.HIGHEST)  3.79 us
  transfers between devices with their start and end apart: 1, of which 1 were waited for; matrix products, arithmetic and copies ran while one was open for 0% of the time, Pallas kernels for 0%

profile of v1, /device:TPU:0, one launch (start us, length us, event | category | flops | bytes accessed | tf_op | source)
XLA Modules:
  0.0 135.7 jit_solution(7784066049827033600)
XLA Ops:
  2.2 2.0 %convolution_bitcast_fusion = f32[4,4,256,64]{2,3,1,0:T(8,128)S(1)} fusion(f32[4,4,128,64]{2,3,1,0:T(8,128)S(1)} %copy-done, f32[256]{0:T(256)S(1)} %bitcast.106, s32[256]{0:T(256)S(1)} %get-tuple-element.53, f32[256]{0:T(256)S(1)} %bitcast.107, s32[256]{0:T(256)S(1)} %get-tuple-element.54, f32[256]{0:T(256)S(1)} %bitcast.108, ...), kind=kOutput, calls=%fused_computation.4 | convolution fusion | flops 403013632 | bytes 1581056 | tf_op jit(solution)/shard_map/jb,cibz->cijz/dot_general | solution.py:22
  4.1 3.9 %slice_bitcast_fusion.19 = (f32[1,4,4,8,64]{3,4,2,1,0:T(8,128)}, f32[1,4,4,8,64]{3,4,2,1,0:T(8,128)}, f32[1,4,4,8,64]{3,4,2,1,0:T(8,128)}, f32[1,4,4,8,64]{3,4,2...) fusion(f32[4,4,256,64]{2,3,1,0:T(8,128)S(1)} %convolution_bitca, ...), kind=kLoop, calls=%fused_computation.24 | loop fusion | bytes 851968 | tf_op jit(solution)/shard_map/stack | solution.py:37
  8.0 6.0 %slice_bitcast_fusion = (f32[1,4,4,8,64]{3,4,2,1,0:T(8,128)}, f32[1,4,4,8,64]{3,4,2,1,0:T(8,128)}, f32[1,4,4,8,64]{3,4,2,1,0:T(8,128)}, f32[1,4,4,8,64]{3,4,2,1,...) fusion(f32[4,4,256,64]{2,3,1,0:T(8,128)S(1)} %convolution_bitca, ...), kind=kLoop, calls=%fused_computation.5 | loop fusion | bytes 1245184 | tf_op jit(solution)/shard_map/stack | solution.py:37
  14.0 1.9 %copy.23 = f32[1,4,4,8,64]{4,3,2,1,0:T(8,128)} copy(f32[1,4,4,8,64]{3,4,2,1,0:T(8,128)} %get-tuple-element.24) | data formatting | bytes 65536 | tf_op jit(solution)/shard_map/stack | solution.py:37
  17.7 1.9 %copy.21 = f32[1,4,4,8,64]{4,3,2,1,0:T(8,128)} copy(f32[1,4,4,8,64]{3,4,2,1,0:T(8,128)} %get-tuple-element.26) | data formatting | bytes 65536 | tf_op jit(solution)/shard_map/stack | solution.py:37
  19.6 1.9 %copy.20 = f32[1,4,4,8,64]{4,3,2,1,0:T(8,128)} copy(f32[1,4,4,8,64]{3,4,2,1,0:T(8,128)} %get-tuple-element.27) | data formatting | bytes 65536 | tf_op jit(solution)/shard_map/stack | solution.py:37
  23.3 1.9 %copy.18 = f32[1,4,4,8,64]{4,3,2,1,0:T(8,128)} copy(f32[1,4,4,8,64]{3,4,2,1,0:T(8,128)} %get-tuple-element.29) | data formatting | bytes 65536 | tf_op jit(solution)/shard_map/stack | solution.py:37
  25.2 1.9 %copy.17 = f32[1,4,4,8,64]{4,3,2,1,0:T(8,128)} copy(f32[1,4,4,8,64]{3,4,2,1,0:T(8,128)} %get-tuple-element.30) | data formatting | bytes 65536 | tf_op jit(solution)/shard_map/stack | solution.py:37
  28.9 1.9 %copy.15 = f32[1,4,4,8,64]{4,3,2,1,0:T(8,128)} copy(f32[1,4,4,8,64]{3,4,2,1,0:T(8,128)} %get-tuple-element.32) | data formatting | bytes 65536 | tf_op jit(solution)/shard_map/stack | solution.py:37
  40.7 1.9 %copy.36 = f32[1,4,4,8,64]{4,3,2,1,0:T(8,128)} copy(f32[1,4,4,8,64]{3,4,2,1,0:T(8,128)} %get-tuple-element.11) | data formatting | bytes 65536 | tf_op jit(solution)/shard_map/stack | solution.py:37
  44.4 1.9 %copy.34 = f32[1,4,4,8,64]{4,3,2,1,0:T(8,128)} copy(f32[1,4,4,8,64]{3,4,2,1,0:T(8,128)} %get-tuple-element.13) | data formatting | bytes 65536 | tf_op jit(solution)/shard_map/stack | solution.py:37
  48.1 1.9 %copy.32 = f32[1,4,4,8,64]{4,3,2,1,0:T(8,128)} copy(f32[1,4,4,8,64]{3,4,2,1,0:T(8,128)} %get-tuple-element.15) | data formatting | bytes 65536 | tf_op jit(solution)/shard_map/stack | solution.py:37
  51.8 1.9 %copy.30 = f32[1,4,4,8,64]{4,3,2,1,0:T(8,128)} copy(f32[1,4,4,8,64]{3,4,2,1,0:T(8,128)} %get-tuple-element.17) | data formatting | bytes 65536 | tf_op jit(solution)/shard_map/stack | solution.py:37
  57.4 1.9 %copy.27 = f32[1,4,4,8,64]{4,3,2,1,0:T(8,128)} copy(f32[1,4,4,8,64]{3,4,2,1,0:T(8,128)} %get-tuple-element.20) | data formatting | bytes 65536 | tf_op jit(solution)/shard_map/stack | solution.py:37
  59.2 1.9 %copy.26 = f32[1,4,4,8,64]{4,3,2,1,0:T(8,128)} copy(f32[1,4,4,8,64]{3,4,2,1,0:T(8,128)} %get-tuple-element.21) | data formatting | bytes 65536 | tf_op jit(solution)/shard_map/stack | solution.py:37
  61.1 1.9 %copy.25 = f32[1,4,4,8,64]{4,3,2,1,0:T(8,128)} copy(f32[1,4,4,8,64]{3,4,2,1,0:T(8,128)} %get-tuple-element.22) | data formatting | bytes 65536 | tf_op jit(solution)/shard_map/stack | solution.py:37
  77.8 2.3 %reshape.47 = f32[32,1,8192]{2,1,0:T(1,128)} reshape(f32[32,4,4,8,64]{4,3,2,1,0:T(8,128)S(1)} %constant_dynamic-update-slice_fusion) | data formatting | bytes 2097152
  80.0 7.5 %all-to-all-start = ((f32[32,1,8192]{2,1,0:T(1,128)}), f32[32,1,8192]{2,1,0:T(1,128)S(1)}, u32[]{:S(2)}, u32[]{:S(2)}) async-start(f32[32,1,8192]{2,1,0:T(1,128)} %reshape.47), calls=%async_computation | async-start | bytes 2097152 | tf_op jit(solution)/shard_map/all_to_all | solution.py:36
  87.7 25.9 %all-to-all-done = f32[32,1,8192]{2,1,0:T(1,128)S(1)} async-done(((f32[32,1,8192]{2,1,0:T(1,128)}), f32[32,1,8192]{2,1,0:T(1,128)S(1)}, u32[]{:S(2)}, u32[]{:S(2)}) %all-to-all-start) | async-done | bytes 1048608 | tf_op jit(solution)/shard_map/all_to_all | solution.py:36
  114.1 4.4 %reduce = f32[32,8192]{1,0:T(8,128)} reduce(f32[32,1,8192]{2,1,0:T(1,128)S(1)} %all-to-all-done, f32[]{:T(128)} %broadcast.42), dimensions={1}, to_apply=%all_to_all.3.reduce_sub_computation | reduce | bytes 2097156 | tf_op jit(solution)/shard_map/all_to_all | solution.py:36
  118.5 2.0 %reshape.48 = f32[32,4,4,8,64]{4,3,2,1,0:T(8,128)S(1)} reshape(f32[32,8192]{1,0:T(8,128)} %reduce) | data formatting | bytes 2097152
  120.7 3.8 %fusion.2 = f32[4,8,64,256]{3,2,1,0:T(8,128)S(1)} fusion(f32[4,128,8,64]{3,2,1,0:T(8,128)S(1)} %bitcast.103, f32[256]{0:T(256)S(1)} %bitcast.110, s32[256]{0:T(256)S(1)} %get-tuple-element.50, f32[256]{0:T(256)S(1)} %bitcast.111, s32[256]{0:T(256)S(1)} %get-tuple-element.51, f32[256]{0:T(256)S(1)} %bitcast.112, s32[256]{0:T(256)S(1)} %get-tuple-element.49, ...), kind=kOutput, calls=%fused_computation.2 | convolution fusion | flops 805666816 | bytes 3153920 | tf_op jit(solution)/shard_map/ia,cayz->ciyz/dot_general | solution.py:18
  124.5 6.8 %fusion = f32[4,256,8,128]{3,1,2,0:T(8,128)S(1)} fusion(f32[4,8,64,256]{3,2,1,0:T(8,128)S(1)} %fusion.2, f32[128]{0:T(128)S(1)} %get-tuple-element.46, s32[128]{0:T(128)S(1)} %get-tuple-element.56, f32[128]{0:T(128)S(1)} %get-tuple-element.47, s32[128]{0:T(128)S(1)} %get-tuple-element.57, f32[128]{0:T(128)S(1)} %get-tuple-element.48, ...), kind=kOutput, calls=%fused_computation | convolution fusion | flops 805396480 | bytes 6295552 | tf_op jit(solution)/shard_map/le,cije->cijl/dot_general | solution.py:26
  131.3 4.4 %copy.45 = f32[4,256,8,128]{3,2,1,0:T(8,128)} copy(f32[4,256,8,128]{3,1,2,0:T(8,128)S(1)} %fusion) | data formatting | bytes 8388608 | tf_op jit(solution)/shard_map/le,cije->cijl/dot_general | solution.py:26
  (93 shorter events, 42.3 us)
Async XLA Ops:
  0.0 2.2 %copy-start = (f32[4,4,128,64]{2,3,1,0:T(8,128)S(1)}, f32[4,4,128,64]{2,3,1,0:T(8,128)}, u32[]{:S(2)}) copy-start(f32[4,4,128,64]{2,3,1,0:T(8,128)} %param.7) | copy-start | bytes 1572868
  63.7 13.7 %copy-start.9 = (f32[1,4,4,8,64]{4,3,2,1,0:T(8,128)S(1)}, f32[1,4,4,8,64]{4,3,2,1,0:T(8,128)}, u32[]{:S(2)}) copy-start(f32[1,4,4,8,64]{4,3,2,1,0:T(8,128)} %copy.28) | copy-start | bytes 98308
  63.7 13.7 %copy-start.8 = (f32[1,4,4,8,64]{4,3,2,1,0:T(8,128)S(1)}, f32[1,4,4,8,64]{4,3,2,1,0:T(8,128)}, u32[]{:S(2)}) copy-start(f32[1,4,4,8,64]{4,3,2,1,0:T(8,128)} %copy.29) | copy-start | bytes 98308
  63.7 13.7 %copy-start.7 = (f32[1,4,4,8,64]{4,3,2,1,0:T(8,128)S(1)}, f32[1,4,4,8,64]{4,3,2,1,0:T(8,128)}, u32[]{:S(2)}) copy-start(f32[1,4,4,8,64]{4,3,2,1,0:T(8,128)} %copy.30) | copy-start | bytes 98308
  63.7 13.7 %copy-start.6 = (f32[1,4,4,8,64]{4,3,2,1,0:T(8,128)S(1)}, f32[1,4,4,8,64]{4,3,2,1,0:T(8,128)}, u32[]{:S(2)}) copy-start(f32[1,4,4,8,64]{4,3,2,1,0:T(8,128)} %copy.31) | copy-start | bytes 98308
  63.7 13.7 %copy-start.5 = (f32[1,4,4,8,64]{4,3,2,1,0:T(8,128)S(1)}, f32[1,4,4,8,64]{4,3,2,1,0:T(8,128)}, u32[]{:S(2)}) copy-start(f32[1,4,4,8,64]{4,3,2,1,0:T(8,128)} %copy.32) | copy-start | bytes 98308
  63.8 13.8 %copy-start.4 = (f32[1,4,4,8,64]{4,3,2,1,0:T(8,128)S(1)}, f32[1,4,4,8,64]{4,3,2,1,0:T(8,128)}, u32[]{:S(2)}) copy-start(f32[1,4,4,8,64]{4,3,2,1,0:T(8,128)} %copy.33) | copy-start | bytes 98308
  63.8 13.8 %copy-start.3 = (f32[1,4,4,8,64]{4,3,2,1,0:T(8,128)S(1)}, f32[1,4,4,8,64]{4,3,2,1,0:T(8,128)}, u32[]{:S(2)}) copy-start(f32[1,4,4,8,64]{4,3,2,1,0:T(8,128)} %copy.34) | copy-start | bytes 98308
  63.8 13.8 %copy-start.2 = (f32[1,4,4,8,64]{4,3,2,1,0:T(8,128)S(1)}, f32[1,4,4,8,64]{4,3,2,1,0:T(8,128)}, u32[]{:S(2)}) copy-start(f32[1,4,4,8,64]{4,3,2,1,0:T(8,128)} %copy.35) | copy-start | bytes 98308
  63.8 13.8 %copy-start.1 = (f32[1,4,4,8,64]{4,3,2,1,0:T(8,128)S(1)}, f32[1,4,4,8,64]{4,3,2,1,0:T(8,128)}, u32[]{:S(2)}) copy-start(f32[1,4,4,8,64]{4,3,2,1,0:T(8,128)} %copy.36) | copy-start | bytes 98308
  77.7 9.8 %copy-start.11 = (f32[4,128]{1,0:T(4,128)S(1)}, f32[4,128]{1,0:T(4,128)}, u32[]{:S(2)}) copy-start(f32[4,128]{1,0:T(4,128)} %param.13) | copy-start | bytes 6148
  77.7 9.8 %copy-start.10 = (f32[4,256]{1,0:T(4,128)S(1)}, f32[4,256]{1,0:T(4,128)}, u32[]{:S(2)}) copy-start(f32[4,256]{1,0:T(4,128)} %param.9) | copy-start | bytes 12292
  77.7 9.9 %copy-start.13 = (s32[128]{0:T(128)S(1)}, s32[128]{0:T(128)}, u32[]{:S(2)}) copy-start(s32[128]{0:T(128)} %param.12) | copy-start | bytes 1540
  77.7 9.9 %copy-start.12 = (s32[256]{0:T(256)S(1)}, s32[256]{0:T(256)}, u32[]{:S(2)}) copy-start(s32[256]{0:T(256)} %param.8) | copy-start | bytes 3076
  80.0 33.5 %all-to-all-start = ((f32[32,1,8192]{2,1,0:T(1,128)}), f32[32,1,8192]{2,1,0:T(1,128)S(1)}, u32[]{:S(2)}, u32[]{:S(2)}) async-start(f32[32,1,8192]{2,1,0:T(1,128)} %reshape.47), calls=%async_computation | async-start | bytes 2097152 | tf_op jit(solution)/shard_map/all_to_all | solution.py:36
